TPU v7x, 512 devices: a whole 4x8x8 slice. The times are simulated.
512 devices in a mesh: dp: 8 (over z), fsdp: 64 (over y, x, core).
Axes of the slice: x: 4, y: 8, z: 8, core: 2. Of those that a mesh axis runs over, the one named last changes fastest.
Arguments:
- small_cols: bfloat16 [393216, 128], P(('dp', 'fsdp')), may hold values from -24 to 24
- wide_cols: bfloat16 [393216, 2, 1536], P(('dp', 'fsdp')), may hold values from -24 to 24
- token_counts: int32 [512], P(('dp', 'fsdp')), may hold values from 144 to 768, as said below
- loss_sums: float32 [512], P(('dp', 'fsdp'))
- weight: float32 [128, 1536], P('fsdp'), may hold values from -0.75 to 0.75
- first_moment: float32 [128, 1536], P('fsdp'), may hold values from -0.002 to 0.002
- second_moment: float32 [128, 1536], P('fsdp'), may hold values from 1e-07 to 1e-06
- step: int32 [], replicated, may hold values from 1 to 2999
Outputs:
- new_weight: float32 [128, 1536], P('fsdp')
- new_first: float32 [128, 1536], P('fsdp')
- new_second: float32 [128, 1536], P('fsdp')
- adam_step: float32 [128, 1536], P('fsdp')
- grad_norm: float32 [], replicated
- mean_loss: float32 [], replicated
Inputs may be any that keep to these rules, and one draw needn't show every extreme that they name: `token_counts`: each count is f * h * w with f from 1 to 3 and h, w from 12 to 16; in every draw some device's count is exactly 768.
All inputs are finite; a program needn't handle non-finite values.
Results may differ from a plain program's by a relative error of at most 0.0003.
Values sent between devices are 32-bit elements; how exact they have to be, the bound alone decides.
No kernel may reach another device: no remote copies, remote signals or barrier semaphores. Data moves between devices by JAX's collectives and lax.ppermute only.
A program may use at most 64 MiB of HBM per device.

v0:
```python
import jax
import jax.numpy as jnp
from jax import lax
from jax.sharding import PartitionSpec as P

MAX_NORM = 1.0
BETA_FIRST = 0.9
BETA_SECOND = 0.999
EPSILON_ADAM = 1e-08
LEARN_RATE = 0.02
DECAY_RATE = 0.1


def in_blocks(array, dim, peers):
    lengths = array.shape
    parts = array.reshape(*lengths[:dim], peers, lengths[dim] // peers, *lengths[dim + 1 :])
    return jnp.moveaxis(parts, dim, 0)


def sum_at_owner(array, axis, dim):
    peers = lax.axis_size(axis)
    parts = lax.all_to_all(in_blocks(array, dim, peers), axis, 0, 0, tiled=True)
    return jnp.sum(parts, axis=0)


def from_everyone(array, axis):
    peers = lax.axis_size(axis)
    return lax.all_to_all(
        jnp.broadcast_to(array[None], (peers, *array.shape)), axis, 0, 0, tiled=True
    )


def taken_together(array, axis):
    everything = from_everyone(array, axis)
    return jnp.sum(everything, axis=0)


def in_one(arrays, axis):
    ends = [0]
    for a in arrays:
        ends.append(ends[-1] + a.size)
    total = taken_together(jnp.concatenate([a.ravel() for a in arrays]), axis)
    return tuple((total[b:e].reshape(a.shape) for a, b, e in zip(arrays, ends, ends[1:])))


def slot_product(narrow, broad, live_count):
    block_rows = narrow.shape[0]
    half_cols = narrow.shape[1] // 2
    is_live = jnp.arange(block_rows, dtype=jnp.int32) < live_count
    narrow = jnp.where(is_live[:, None], narrow, jnp.zeros_like(narrow))
    portion = jnp.einsum(
        "thc,thd->hcd",
        narrow.reshape(block_rows, 2, half_cols),
        broad,
        preferred_element_type=jnp.float32,
    )
    return portion.reshape(2 * half_cols, broad.shape[2])


def device_term(small_cols, wide_cols, live_count):
    return slot_product(small_cols, wide_cols, live_count)


def on_device(
    small_cols, wide_cols, token_counts, loss_sums, weight, first_moment, second_moment, step
):
    live_count = token_counts[0]
    contribution = device_term(small_cols, wide_cols, live_count)
    count_float = token_counts.astype(jnp.float32)[0]
    loss_local = loss_sums[0]
    owned_sum = sum_at_owner(contribution, "fsdp", 0)
    summed, count_groups, loss_groups = in_one((owned_sum, count_float, loss_local), "dp")
    squares, token_total, loss_total = in_one(
        (jnp.sum(summed * summed), count_groups, loss_groups), "fsdp"
    )
    gradient = summed / token_total
    grad_norm = jnp.sqrt(squares) / token_total
    mean_loss = loss_total / token_total
    clip_factor = jnp.minimum(1.0, MAX_NORM / (grad_norm + 1e-06))
    clipped = gradient * clip_factor
    new_first = BETA_FIRST * first_moment + (1.0 - BETA_FIRST) * clipped
    new_second = BETA_SECOND * second_moment + (1.0 - BETA_SECOND) * clipped * clipped
    step_float = step.astype(jnp.float32)
    first_hat = new_first / (1.0 - jnp.power(jnp.float32(BETA_FIRST), step_float))
    second_hat = new_second / (1.0 - jnp.power(jnp.float32(BETA_SECOND), step_float))
    adam_step = first_hat / (jnp.sqrt(second_hat) + EPSILON_ADAM) + DECAY_RATE * weight
    new_weight = weight - LEARN_RATE * adam_step
    return (new_weight, new_first, new_second, adam_step, grad_norm, mean_loss)


def solution(mesh):
    in_specs = (
        P(("dp", "fsdp"), None),
        P(("dp", "fsdp"), None, None),
        P(("dp", "fsdp")),
        P(("dp", "fsdp")),
        P("fsdp", None),
        P("fsdp", None),
        P("fsdp", None),
        P(),
    )
    out_specs = (P("fsdp", None), P("fsdp", None), P("fsdp", None), P("fsdp", None), P(), P())
    return jax.shard_map(
        on_device, mesh=mesh, in_specs=in_specs, out_specs=out_specs, check_vma=False
    )
```

profile of v0, /device:TPU:1, one launch (start us, length us, event | category | flops | bytes accessed | tf_op | source)
XLA Modules:
  0.0 85.4 jit_solution(13052749407866836515)
XLA Ops:
  1.3 1.1 %copy.24 = bf16[768,128]{0,1:T(8,128)(2,1)S(1)} copy(bf16[768,128]{1,0:T(8,128)(2,1)} %param.8) | data formatting | bytes 393216 | tf_op args[0]
  2.4 0.0 copy-start
  2.4 0.0 copy-start.1
  2.4 0.0 copy-start.2
  2.4 3.3 %fusion = f32[2,64,1536]{2,1,0:T(8,128)S(1)} fusion(bf16[768,2,64]{0,2,1:T(8,128)(2,1)S(1)} %bitcast.8, bf16[768,2,1536]{2,1,0:T(2,128)(2,1)} %param.9), kind=kOutput, calls=%fused_computation | convolution fusion | flops 301989888 | bytes 5701632 | tf_op jit(solution)/shard_map/thc,thd->hcd/dot_general | solution.py:51
  5.7 1.3 %reshape_reshape.3 = f32[64,2,1536]{2,1,0:T(2,128)} reshape(f32[2,64,1536]{2,1,0:T(8,128)S(1)} %fusion) | data formatting | bytes 1572864 | tf_op jit(solution)/shard_map/reshape;reshape | solution.py:16
  7.0 11.6 %all-to-all-start = ((f32[64,2,1536]{2,1,0:T(2,128)}), f32[64,2,1536]{2,1,0:T(2,128)S(1)}, u32[]{:S(2)}, u32[]{:S(2)}) async-start(f32[64,2,1536]{2,1,0:T(2,128)} %reshape_reshape.3), calls=%async_computation | async-start | bytes 1572864 | tf_op jit(solution)/shard_map/all_to_all | solution.py:22
  19.3 22.4 %all-to-all-done = f32[64,2,1536]{2,1,0:T(2,128)S(1)} async-done(((f32[64,2,1536]{2,1,0:T(2,128)}), f32[64,2,1536]{2,1,0:T(2,128)S(1)}, u32[]{:S(2)}, u32[]{:S(2)}) %all-to-all-start) | async-done | bytes 786464 | tf_op jit(solution)/shard_map/all_to_all | solution.py:22
  41.7 0.3 reduce_sum.36
  41.9 0.1 concatenate.7
  42.0 0.1 broadcast_in_dim.26
  42.1 17.5 %all_to_all.17 = f32[8,1,3074]{2,1,0:T(1,128)S(1)} all-to-all(f32[8,1,3074]{2,1,0:T(1,128)S(1)} %broadcast_in_dim.26), channel_id=1, replica_groups=mesh['dp'=8,'fsdp'=64] {'dp'}, dimensions={0} | all-to-all | bytes 196736 | tf_op jit(solution)/shard_map/all_to_all | solution.py:28
  59.6 0.1 reduce_sum.37
  59.6 0.6 multiply_reduce_fusion
  60.3 0.7 pad_maximum_fusion
  61.0 0.6 broadcast_in_dim.27
  61.6 7.3 %all-to-all-start.2 = ((f32[64,1,3]{2,1,0:T(1,128)}), f32[64,1,3]{2,1,0:T(1,128)S(1)}, u32[]{:S(2)}, u32[]{:S(2)}) async-start(f32[64,1,3]{2,1,0:T(1,128)} %broadcast_in_dim.27), calls=%async_computation.2 | async-start | bytes 65536 | tf_op jit(solution)/shard_map/all_to_all | solution.py:28
  69.6 8.7 %all-to-all-done.2 = f32[64,1,3]{2,1,0:T(1,128)S(1)} async-done(((f32[64,1,3]{2,1,0:T(1,128)}), f32[64,1,3]{2,1,0:T(1,128)S(1)}, u32[]{:S(2)}, u32[]{:S(2)}) %all-to-all-start.2) | async-done | bytes 800 | tf_op jit(solution)/shard_map/all_to_all | solution.py:28
  78.3 0.1 reduce_sum.39
  78.4 0.6 fusion.4
  80.4 0.7 divide_multiply_fusion
  82.4 0.0 copy-done
  82.4 0.0 copy-done.1
  82.5 0.7 multiply_subtract_fusion
  (6 shorter events, 0.1 us)
Async XLA Ops:
  2.4 80.0 %copy-start = (f32[2,1536]{1,0:T(2,128)S(1)}, f32[2,1536]{1,0:T(2,128)}, u32[]{:S(2)}) copy-start(f32[2,1536]{1,0:T(2,128)} %param.12) | copy-start | bytes 36868
  2.4 80.0 %copy-start.1 = (f32[2,1536]{1,0:T(2,128)S(1)}, f32[2,1536]{1,0:T(2,128)}, u32[]{:S(2)}) copy-start(f32[2,1536]{1,0:T(2,128)} %param.14) | copy-start | bytes 36868
  2.4 80.0 %copy-start.2 = (f32[2,1536]{1,0:T(2,128)S(1)}, f32[2,1536]{1,0:T(2,128)}, u32[]{:S(2)}) copy-start(f32[2,1536]{1,0:T(2,128)} %param.13) | copy-start | bytes 36868
  7.0 34.6 %all-to-all-start = ((f32[64,2,1536]{2,1,0:T(2,128)}), f32[64,2,1536]{2,1,0:T(2,128)S(1)}, u32[]{:S(2)}, u32[]{:S(2)}) async-start(f32[64,2,1536]{2,1,0:T(2,128)} %reshape_reshape.3), calls=%async_computation | async-start | bytes 1572864 | tf_op jit(solution)/shard_map/all_to_all | solution.py:22
  61.6 16.7 %all-to-all-start.2 = ((f32[64,1,3]{2,1,0:T(1,128)}), f32[64,1,3]{2,1,0:T(1,128)S(1)}, u32[]{:S(2)}, u32[]{:S(2)}) async-start(f32[64,1,3]{2,1,0:T(1,128)} %broadcast_in_dim.27), calls=%async_computation.2 | async-start | bytes 65536 | tf_op jit(solution)/shard_map/all_to_all | solution.py:28
where the time goes:
time: 85.8 us; the launch traced here: 85.4 us
  waiting for transfers between devices  31 us (36%)
  starting transfers between devices  18.9 us (22%)
  blocking collectives  17.5 us (20%)
  between operations  7.79 us (9%)
  local copies, waits for them, and re-layouts  3.8 us (4%)
  matrix products  3.28 us (4%)
  other arithmetic  3.08 us (4%)
    all_to_all x1, waiting for transfers between devices, sum_at_owner(): parts = lax.all_to_all(in_blocks(array, dim, peers), axis, 0, 0, tiled=True)  22.4 us
    all_to_all x1, blocking collectives, from_everyone(): lax.all_to_all(jnp.broadcast_to(array[None], (peers, *array.shape)), axis...  17.5 us
    all_to_all x1, starting transfers between devices, sum_at_owner(): parts = lax.all_to_all(in_blocks(array, dim, peers), axis, 0, 0, tiled=True)  11.6 us
    all_to_all x1, waiting for transfers between devices, from_everyone(): lax.all_to_all(jnp.broadcast_to(array[None], (peers, *array.shape)), axis...  8.67 us
    all_to_all x1, starting transfers between devices, from_everyone(): lax.all_to_all(jnp.broadcast_to(array[None], (peers, *array.shape)), axis...  7.31 us
    dot_general x1, matrix products, slot_product(): jnp.einsum('thc,thd->hcd', narrow.reshape(block_rows, 2, half_cols), broa...  3.28 us
  transfers between devices with their start and end apart: 2, of which 2 were waited for; matrix products, arithmetic and copies ran while one was open for 0% of the time, Pallas kernels for 0%

commit v1 on v0

v1 whole, which is shorter than its diff:
```python
import functools
import math

import jax
import jax.numpy as jnp
from jax import lax
from jax.experimental import pallas as pl
from jax.experimental.pallas import tpu as pltpu
from jax.sharding import PartitionSpec as P

MAX_NORM = 1.0
BETA_FIRST = 0.9
BETA_SECOND = 0.999
EPSILON_ADAM = 1e-08
LEARN_RATE = 0.02
DECAY_RATE = 0.1
LOG_FIRST = -0.10536054214877988
LOG_SECOND = -0.0010004874460928543

LANES = 128
STEP_TOKENS = 128
VMEM = pl.BlockSpec(memory_space=pltpu.VMEM)
HBM = pl.BlockSpec(memory_space=pltpu.HBM)
ANY = pl.BlockSpec(memory_space=pl.ANY)


def in_hbm(array):
    return pltpu.with_memory_space_constraint(array, pltpu.HBM)


def correction(step, log_beta):
    u = step * log_beta
    series = jnp.ones_like(u)
    for k in range(11, 1, -1):
        series = 1.0 + (u / k) * series
    return jnp.where(u > -0.5, -u * series, 1.0 - jnp.exp(u))


def term_kernel(
    count_ref,
    loss_ref,
    step_ref,
    small_ref,
    wide_ref,
    keep_ref,
    send_ref,
    extra_ref,
    small_vmem,
    wide_vmem,
    total,
    count_held,
    loss_held,
    step_held,
    sems,
    small_sems,
):
    tokens, width = small_ref.shape
    steps = sems.shape[0]
    each = tokens // steps
    core = lax.rem(lax.axis_index("fsdp"), 2)
    first = [
        pltpu.make_async_copy(ref, held, small_sems.at[i])
        for i, (ref, held) in enumerate(
            (
                (count_ref, count_held),
                (small_ref, small_vmem),
                (loss_ref, loss_held),
                (step_ref, step_held),
            )
        )
    ]
    copies = [
        pltpu.make_async_copy(
            wide_ref.at[pl.ds(i * each, each)], wide_vmem.at[pl.ds(i * each, each)], sems.at[i]
        )
        for i in range(steps)
    ]
    for c in first[:2] + copies + first[2:]:
        c.start()
    first[0].wait()
    live = count_held[...]
    first[1].wait()
    tiles = total.shape[0]
    for i in range(steps):
        copies[i].wait()
        row = lax.broadcasted_iota(jnp.int32, (2 * each, each), 0)
        col = lax.broadcasted_iota(jnp.int32, (2 * each, each), 1)
        twice = jnp.where((row // 2 == col) & (col + i * each < live), 1.0, 0.0).astype(jnp.bfloat16)
        narrow = jnp.dot(
            twice, small_vmem[i * each : (i + 1) * each, :], preferred_element_type=jnp.float32
        )
        row = lax.broadcasted_iota(jnp.int32, (2 * each, width), 0)
        col = lax.broadcasted_iota(jnp.int32, (2 * each, width), 1)
        narrow = jnp.where(row % 2 == col // (width // 2), narrow, 0.0).astype(jnp.bfloat16)
        broad = wide_vmem[i * each : (i + 1) * each].reshape(2 * each, tiles * LANES)
        term = lax.dot_general(
            narrow, broad, (((0,), (0,)), ((), ())), preferred_element_type=jnp.float32
        )
        for t in range(tiles):
            part = term[:, t * LANES : (t + 1) * LANES]
            total[t] = part if i == 0 else total[t] + part
    first[2].wait()
    first[3].wait()
    lane = lax.broadcasted_iota(jnp.int32, (1, LANES), 1)
    step = step_held[...].astype(jnp.float32)
    scales = correction(step, jnp.where(lane == 3, LOG_FIRST, LOG_SECOND))
    extra = jnp.where(lane == 0, live.astype(jnp.float32), jnp.where(lane == 1, loss_held[...], scales))
    extra_ref[...] = jnp.broadcast_to(extra, extra_ref.shape)
    owners = keep_ref.shape[0]
    for t in range(tiles):
        for j in range(2):
            even = total[t, pl.ds(j, owners, stride=4), :]
            odd = total[t, pl.ds(2 + j, owners, stride=4), :]
            keep_ref[:, 2 * t + j, :] = jnp.where(core == 0, even, odd)
            send_ref[:, 2 * t + j, :] = jnp.where(core == 0, odd, even)


def device_term(small_cols, wide_cols, token_counts, loss_sums, step):
    tokens, width = small_cols.shape
    d = wide_cols.shape[2]
    half = jax.ShapeDtypeStruct((width // 4, 2 * d // LANES, LANES), jnp.float32)
    return pl.pallas_call(
        term_kernel,
        out_shape=(half, half, jax.ShapeDtypeStruct((8, LANES), jnp.float32)),
        in_specs=[ANY] * 3 + [HBM] * 2,
        out_specs=(VMEM, VMEM, VMEM),
        scratch_shapes=[
            pltpu.VMEM((tokens, width), jnp.bfloat16),
            pltpu.VMEM((tokens, 2, d), jnp.bfloat16),
            pltpu.VMEM((d // LANES, width, LANES), jnp.float32),
            pltpu.VMEM((1, 1), jnp.int32),
            pltpu.VMEM((1, 1), jnp.float32),
            pltpu.VMEM((1, 1), jnp.int32),
            pltpu.SemaphoreType.DMA((tokens // STEP_TOKENS,)),
            pltpu.SemaphoreType.DMA((4,)),
        ],
        compiler_params=pltpu.CompilerParams(vmem_limit_bytes=16 * 2**20),
        name="term",
    )(*(a.reshape(1, 1) for a in (token_counts, loss_sums, step)), in_hbm(small_cols), in_hbm(wide_cols))


def owned_kernel(extra_ref, parts_ref, out_ref):
    rows = parts_ref.shape[1]
    total = jnp.sum(parts_ref[...], axis=0)
    extra = extra_ref[...]
    for k in range(out_ref.shape[0]):
        out_ref[k, 0:rows, :] = total
        out_ref[k, rows:, :] = extra


def owned(extra, parts, replicas):
    rows = parts.shape[1] + extra.shape[0]
    return pl.pallas_call(
        owned_kernel,
        out_shape=jax.ShapeDtypeStruct((replicas, rows, LANES), jnp.float32),
        in_specs=[VMEM, VMEM],
        out_specs=VMEM,
        compiler_params=pltpu.CompilerParams(vmem_limit_bytes=4 * 2**20),
        name="owned",
    )(extra, parts)


def square_kernel(parts_ref, summed_ref, message_ref):
    rows = summed_ref.shape[0]
    total = jnp.sum(parts_ref[...], axis=0)
    summed = total[:rows]
    summed_ref[...] = summed
    squares = jnp.sum(summed * summed)
    lane = lax.broadcasted_iota(jnp.int32, (1, LANES), 1)
    shifted = total[rows : rows + 1]
    message = jnp.where(lane == 2, squares, shifted)
    message_ref[...] = jnp.broadcast_to(message, message_ref.shape)


def square(parts, owners):
    rows = parts.shape[1] - 8
    return pl.pallas_call(
        square_kernel,
        out_shape=(
            jax.ShapeDtypeStruct((rows, LANES), jnp.float32),
            jax.ShapeDtypeStruct((owners, LANES), jnp.float32),
        ),
        in_specs=[VMEM],
        out_specs=(VMEM, VMEM),
        compiler_params=pltpu.CompilerParams(vmem_limit_bytes=4 * 2**20),
        name="square",
    )(parts)


def update_kernel(
    extra_ref,
    message_ref,
    summed_ref,
    weight_ref,
    first_ref,
    second_ref,
    new_weight_ref,
    new_first_ref,
    new_second_ref,
    adam_ref,
    norm_ref,
    loss_ref,
    rows_ref,
):
    first_scale, second_scale = extra_ref[0:1, 3:4], extra_ref[0:1, 4:5]
    sums = jnp.sum(message_ref[...], axis=0, keepdims=True)
    lane = lax.broadcasted_iota(jnp.int32, sums.shape, 1)

    def take(k):
        return jnp.sum(jnp.where(lane == k, sums, 0.0), axis=1, keepdims=True)

    token_total, loss_total, squares = take(0), take(1), take(2)
    grad_norm = jnp.sqrt(squares) / token_total
    clip = jnp.minimum(1.0, MAX_NORM / (grad_norm + 1e-06))
    norm_ref[...] = grad_norm
    loss_ref[...] = loss_total / token_total
    for t in range(rows_ref.shape[1] // LANES):
        rows_ref[:, t * LANES : (t + 1) * LANES] = summed_ref[2 * t : 2 * t + 2, :]
    clipped = rows_ref[...] / token_total * clip
    new_first = BETA_FIRST * first_ref[...] + (1.0 - BETA_FIRST) * clipped
    new_second = BETA_SECOND * second_ref[...] + (1.0 - BETA_SECOND) * clipped * clipped
    first_hat = new_first / first_scale
    second_hat = new_second / second_scale
    weight = weight_ref[...]
    adam = first_hat / (jnp.sqrt(second_hat) + EPSILON_ADAM) + DECAY_RATE * weight
    new_weight_ref[...] = weight - LEARN_RATE * adam
    new_first_ref[...] = new_first
    new_second_ref[...] = new_second
    adam_ref[...] = adam


def update(extra, message, summed, weight, first_moment, second_moment):
    state = jax.ShapeDtypeStruct(weight.shape, jnp.float32)
    scalar = jax.ShapeDtypeStruct((1, 1), jnp.float32)
    return pl.pallas_call(
        update_kernel,
        out_shape=(state, state, state, state, scalar, scalar),
        in_specs=[VMEM] * 6,
        out_specs=(VMEM,) * 6,
        scratch_shapes=[pltpu.VMEM(weight.shape, jnp.float32)],
        compiler_params=pltpu.CompilerParams(vmem_limit_bytes=4 * 2**20),
        name="update",
    )(extra, message, summed, weight, first_moment, second_moment)


def on_device(
    small_cols, wide_cols, token_counts, loss_sums, weight, first_moment, second_moment, step
):
    owners, replicas = lax.axis_size("fsdp"), lax.axis_size("dp")
    keep, send, extra = device_term(small_cols, wide_cols, token_counts, loss_sums, step)
    partner = [(i, i ^ 1) for i in range(owners)]
    chip_sum = keep + lax.ppermute(send, "fsdp", partner)
    same_core = [list(range(c, owners, 2)) for c in range(2)]
    parts = lax.all_to_all(chip_sum, "fsdp", 0, 0, axis_index_groups=same_core, tiled=True)
    parts = lax.all_to_all(owned(extra, parts, replicas), "dp", 0, 0, tiled=True)
    summed, message = square(parts, owners)
    message = lax.all_to_all(message[:, None, :], "fsdp", 0, 0, tiled=True)[:, 0, :]
    new_weight, new_first, new_second, adam_step, grad_norm, mean_loss = update(
        extra,
        message,
        summed,
        weight,
        first_moment,
        second_moment,
    )
    return (
        new_weight,
        new_first,
        new_second,
        adam_step,
        grad_norm.reshape(()),
        mean_loss.reshape(()),
    )


def solution(mesh):
    in_specs = (
        P(("dp", "fsdp"), None),
        P(("dp", "fsdp"), None, None),
        P(("dp", "fsdp")),
        P(("dp", "fsdp")),
        P("fsdp", None),
        P("fsdp", None),
        P("fsdp", None),
        P(),
    )
    out_specs = (P("fsdp", None), P("fsdp", None), P("fsdp", None), P("fsdp", None), P(), P())
    return jax.shard_map(
        on_device, mesh=mesh, in_specs=in_specs, out_specs=out_specs, check_vma=False
    )
```

time: 85.8 us -> 72.1 us (0.84)
  blocking collectives: 17.5 us -> 53.2 us
  waiting for transfers between devices: 31 us -> 1.33 us
  starting transfers between devices: 18.9 us -> 8.75 us
  Pallas kernels: 0 us -> 5.76 us
  between operations: 7.79 us -> 2.65 us
  local copies, waits for them, and re-layouts: 3.8 us -> 0.01 us
  matrix products: 3.28 us -> 0 us
  other arithmetic: 3.08 us -> 0.04 us
    all_to_all x1 -> x3, blocking collectives: 17.5 us -> 53.2 us  [the longest x1 18 us: on_device(): lax.all_to_all(chip_sum, 'fsdp', 0, 0, axis_index_groups=same_core, tiled...]
    all_to_all x2 -> x0, waiting for transfers between devices: 31 us -> none  [the longest x1 22.4 us: sum_at_owner(): parts = lax.all_to_all(in_blocks(array, dim, peers), axis, 0, 0, tiled=True)]
    all_to_all x2 -> x0, starting transfers between devices: 18.9 us -> none  [the longest x1 11.6 us: sum_at_owner(): parts = lax.all_to_all(in_blocks(array, dim, peers), axis, 0, 0, tiled=True)]
    ppermute x0 -> x1, starting transfers between devices: none -> 8.75 us  [on_device(): chip_sum = keep + lax.ppermute(send, 'fsdp', partner)]
    pallas_call x0 -> x4, Pallas kernels: none -> 5.76 us  [the longest x1 4.83 us: device_term(): pl.pallas_call(term_kernel, out_shape=(half, half, jax.ShapeDtypeStruct((...]
    dot_general x1 -> x0, matrix products: 3.28 us -> none  [slot_product(): jnp.einsum('thc,thd->hcd', narrow.reshape(block_rows, 2, half_cols), broa...]
    another operation x1 -> x0, local copies, waits for them, and re-layouts: 1.34 us -> none  [in_blocks(): array.reshape(*lengths[:dim], peers, lengths[dim] // peers, *lengths[dim...]
    ppermute x0 -> x1, waiting for transfers between devices: none -> 1.33 us  [on_device(): chip_sum = keep + lax.ppermute(send, 'fsdp', partner)]
  transfers between devices with their start and end apart: 2 -> 1, of which waited for: 2 -> 1; matrix products, arithmetic and copies ran while one was open for 0% -> 0% of each run, Pallas kernels for 0% -> 0%
where the time goes in v1:
time: 72.1 us; the launch traced here: 71.8 us
  blocking collectives  53.2 us (74%)
  starting transfers between devices  8.75 us (12%)
  Pallas kernels  5.76 us (8%)
  between operations  2.65 us (4%)
  waiting for transfers between devices  1.33 us (2%)
    all_to_all x1, blocking collectives, on_device(): lax.all_to_all(chip_sum, 'fsdp', 0, 0, axis_index_groups=same_core, tiled...  18 us
    all_to_all x1, blocking collectives, on_device(): lax.all_to_all(owned(extra, parts, replicas), 'dp', 0, 0, tiled=True)  17.8 us
    all_to_all x1, blocking collectives, on_device(): lax.all_to_all(message[:, None, :], 'fsdp', 0, 0, tiled=True)[:, 0, :]  17.5 us
    ppermute x1, starting transfers between devices, on_device(): chip_sum = keep + lax.ppermute(send, 'fsdp', partner)  8.75 us
    pallas_call x1, Pallas kernels, device_term(): pl.pallas_call(term_kernel, out_shape=(half, half, jax.ShapeDtypeStruct((...  4.83 us
  transfers between devices with their start and end apart: 1, of which 1 were waited for; matrix products, arithmetic and copies ran while one was open for 0% of the time, Pallas kernels for 0%

profile of v1, /device:TPU:1, one launch (start us, length us, event | category | flops | bytes accessed | tf_op | source)
XLA Modules:
  0.0 71.8 jit_solution(10487115711494270417)
XLA Ops:
  0.6 0.0 copy-start.2
  0.6 0.0 copy-start.1
  0.7 0.0 copy-start
  2.6 4.8 %term.1 = (f32[32,24,128]{2,1,0:T(8,128)S(1)}, f32[32,24,128]{2,1,0:T(8,128)S(1)}, f32[8,128]{1,0:T(8,128)S(1)}) custom-call(s32[1,1]{1,0:T(1,128)} %bitcast.9.count_ref, f32[1,1]{1,0:T(1,128)} %bitcast.10.loss_ref, s32[1,1]{1,0:T(1,128)} %bitcast.11.step_ref, bf16[768,128]{1,0:T(8,128)(2,1)} %small_ref.1, bf16[768,2,1536]{2,1,0:T(2,128)(2,1)} %wide_ref.1), custom_call_target="tpu_custom_call" | custom-call | tf_op jit(solution)/shard_map/term/pallas_call | solution.py:122
  7.5 8.7 %collective-permute-start = (f32[32,24,128]{2,1,0:T(8,128)S(1)}, f32[32,24,128]{2,1,0:T(8,128)S(1)}, u32[]{:S(2)}, u32[]{:S(2)}) collective-permute-start(f32[32,24,128]{2,1,0:T(8,128)S(1)} %get-tuple-element.19), channel_id=1, source_target_pairs={{0,1},{1,0},{2,3},{3,2},{4,5},{5,4},{6,7},{7,6},{8,9},{9,8},{10,11... | collective-permute-start | bytes 1179656 | tf_op jit(solution)/shard_map/ppermute | solution.py:252
  16.2 1.3 %collective-permute-done = f32[32,24,128]{2,1,0:T(8,128)S(1)} collective-permute-done((f32[32,24,128]{2,1,0:T(8,128)S(1)}, f32[32,24,128]{2,1,0:T(8,128)S(1)}, u32[]{:S(2)}, u32[]{:S(2)}) %collective-permute-start) | collective-permute-done | bytes 393248 | tf_op jit(solution)/shard_map/ppermute | solution.py:252
  17.6 18.0 %all_to_all.15.parts_ref = f32[32,24,128]{2,1,0:T(8,128)S(1)} all-to-all(f32[32,24,128]{2,1,0:T(8,128)S(1)} %add.3), channel_id=1, replica_groups={{0,2,4,6,8,10,12,14,16,18,20,22,24,26,28,30,32,34,36,38,40,42,44,46,48,..., dimensions={0} | all-to-all | bytes 786432 | tf_op jit(solution)/shard_map/all_to_all | solution.py:254
  35.6 17.8 %all_to_all.16.parts_ref = f32[8,32,128]{2,1,0:T(8,128)S(1)} all-to-all(f32[8,32,128]{2,1,0:T(8,128)S(1)} %owned.1), channel_id=1, replica_groups=mesh['dp'=8,'fsdp'=64] {'dp'}, dimensions={0} | all-to-all | bytes 262144 | tf_op jit(solution)/shard_map/all_to_all | solution.py:255
  53.4 0.1 square.1
  53.5 17.5 %all_to_all.17 = f32[64,1,128]{2,1,0:T(1,128)S(1)} all-to-all(f32[64,1,128]{2,1,0:T(1,128)S(1)} %bitcast.13), channel_id=1, replica_groups=mesh['dp'=8,'fsdp'=64] {'fsdp'}, dimensions={0} | all-to-all | bytes 65536 | tf_op jit(solution)/shard_map/all_to_all | solution.py:257
  71.0 0.0 copy-done.2
  71.0 0.0 copy-done.1
  71.0 0.0 copy-done
  71.0 0.8 %update.1 = (f32[2,1536]{1,0:T(2,128)}, f32[2,1536]{1,0:T(2,128)}, f32[2,1536]{1,0:T(2,128)}, f32[2,1536]{1,0:T(2,128)}, f32[1,1]{1,0:T(1,128)}, /*index=5*/f32[1,1]{1,0:T(1,128)}) custom-call(f32[8,128]{1,0:T(8,128)S(1)} %get-tuple-element.17.extra_ref, f32[64,128]{1,0:T(8,128)S(1)} %bitcast.12, f32[24,128]{1,0:T(8,128)S(1)} %get-tuple-element.21.summed_ref, ...), custom_call_target="tpu_custom_call" | custom-call | tf_op jit(solution)/shard_map/update/pallas_call | solution.py:235
  (2 shorter events, 0.1 us)
Async XLA Ops:
  0.6 70.4 %copy-start.2 = (f32[2,1536]{1,0:T(2,128)S(1)}, f32[2,1536]{1,0:T(2,128)}, u32[]{:S(2)}) copy-start(f32[2,1536]{1,0:T(2,128)} %second_ref.1) | copy-start | bytes 36868
  0.6 70.4 %copy-start.1 = (f32[2,1536]{1,0:T(2,128)S(1)}, f32[2,1536]{1,0:T(2,128)}, u32[]{:S(2)}) copy-start(f32[2,1536]{1,0:T(2,128)} %first_ref.1) | copy-start | bytes 36868
  0.7 70.4 %copy-start = (f32[2,1536]{1,0:T(2,128)S(1)}, f32[2,1536]{1,0:T(2,128)}, u32[]{:S(2)}) copy-start(f32[2,1536]{1,0:T(2,128)} %weight_ref.1) | copy-start | bytes 36868
  7.5 10.1 %collective-permute-start = (f32[32,24,128]{2,1,0:T(8,128)S(1)}, f32[32,24,128]{2,1,0:T(8,128)S(1)}, u32[]{:S(2)}, u32[]{:S(2)}) collective-permute-start(f32[32,24,128]{2,1,0:T(8,128)S(1)} %get-tuple-element.19), channel_id=1, source_target_pairs={{0,1},{1,0},{2,3},{3,2},{4,5},{5,4},{6,7},{7,6},{8,9},{9,8},{10,11... | collective-permute-start | bytes 1179656 | tf_op jit(solution)/shard_map/ppermute | solution.py:252

commit v2 on v1

--- a/solution.py
+++ b/solution.py
@@ -18,94 +18,70 @@
 LOG_SECOND = -0.0010004874460928543
 
 LANES = 128
-STEP_TOKENS = 128
+STEP_TOKENS = 384
 VMEM = pl.BlockSpec(memory_space=pltpu.VMEM)
 HBM = pl.BlockSpec(memory_space=pltpu.HBM)
-ANY = pl.BlockSpec(memory_space=pl.ANY)
+SMEM = pl.BlockSpec(memory_space=pltpu.SMEM)
 
 
 def in_hbm(array):
     return pltpu.with_memory_space_constraint(array, pltpu.HBM)
 
 
-def correction(step, log_beta):
-    u = step * log_beta
-    series = jnp.ones_like(u)
-    for k in range(11, 1, -1):
-        series = 1.0 + (u / k) * series
-    return jnp.where(u > -0.5, -u * series, 1.0 - jnp.exp(u))
-
-
 def term_kernel(
     count_ref,
-    loss_ref,
-    step_ref,
     small_ref,
     wide_ref,
     keep_ref,
     send_ref,
-    extra_ref,
     small_vmem,
     wide_vmem,
+    narrow,
     total,
-    count_held,
-    loss_held,
-    step_held,
     sems,
-    small_sems,
+    small_sem,
 ):
     tokens, width = small_ref.shape
     steps = sems.shape[0]
     each = tokens // steps
     core = lax.rem(lax.axis_index("fsdp"), 2)
-    first = [
-        pltpu.make_async_copy(ref, held, small_sems.at[i])
-        for i, (ref, held) in enumerate(
-            (
-                (count_ref, count_held),
-                (small_ref, small_vmem),
-                (loss_ref, loss_held),
-                (step_ref, step_held),
-            )
-        )
-    ]
+    small_copy = pltpu.make_async_copy(small_ref, small_vmem, small_sem)
     copies = [
         pltpu.make_async_copy(
             wide_ref.at[pl.ds(i * each, each)], wide_vmem.at[pl.ds(i * each, each)], sems.at[i]
         )
         for i in range(steps)
     ]
-    for c in first[:2] + copies + first[2:]:
+    small_copy.start()
+    for c in copies:
         c.start()
-    first[0].wait()
-    live = count_held[...]
-    first[1].wait()
+    live = count_ref[0]
+    small_copy.wait()
+    block = 128
+    for i in range(tokens // block):
+        token = lax.broadcasted_iota(jnp.int32, (block, 2 * block), 0)
+        slot = lax.broadcasted_iota(jnp.int32, (block, 2 * block), 1)
+        twice = jnp.where((slot // 2 == token) & (token + i * block < live), 1.0, 0.0)
+        rows = lax.dot_general(
+            small_vmem[i * block : (i + 1) * block, :],
+            twice.astype(jnp.bfloat16),
+            (((0,), (0,)), ((), ())),
+            preferred_element_type=jnp.float32,
+        )
+        row = lax.broadcasted_iota(jnp.int32, (width, 2 * block), 0)
+        slot = lax.broadcasted_iota(jnp.int32, (width, 2 * block), 1)
+        rows = jnp.where(slot % 2 == row // (width // 2), rows, 0.0)
+        narrow[:, 2 * block * i : 2 * block * (i + 1)] = rows.astype(jnp.bfloat16)
     tiles = total.shape[0]
     for i in range(steps):
         copies[i].wait()
-        row = lax.broadcasted_iota(jnp.int32, (2 * each, each), 0)
-        col = lax.broadcasted_iota(jnp.int32, (2 * each, each), 1)
-        twice = jnp.where((row // 2 == col) & (col + i * each < live), 1.0, 0.0).astype(jnp.bfloat16)
-        narrow = jnp.dot(
-            twice, small_vmem[i * each : (i + 1) * each, :], preferred_element_type=jnp.float32
-        )
-        row = lax.broadcasted_iota(jnp.int32, (2 * each, width), 0)
-        col = lax.broadcasted_iota(jnp.int32, (2 * each, width), 1)
-        narrow = jnp.where(row % 2 == col // (width // 2), narrow, 0.0).astype(jnp.bfloat16)
         broad = wide_vmem[i * each : (i + 1) * each].reshape(2 * each, tiles * LANES)
-        term = lax.dot_general(
-            narrow, broad, (((0,), (0,)), ((), ())), preferred_element_type=jnp.float32
+        term = jnp.dot(
+            narrow[:, 2 * each * i : 2 * each * (i + 1)], broad, preferred_element_type=jnp.float32
         )
         for t in range(tiles):
             part = term[:, t * LANES : (t + 1) * LANES]
             total[t] = part if i == 0 else total[t] + part
-    first[2].wait()
-    first[3].wait()
-    lane = lax.broadcasted_iota(jnp.int32, (1, LANES), 1)
-    step = step_held[...].astype(jnp.float32)
-    scales = correction(step, jnp.where(lane == 3, LOG_FIRST, LOG_SECOND))
-    extra = jnp.where(lane == 0, live.astype(jnp.float32), jnp.where(lane == 1, loss_held[...], scales))
-    extra_ref[...] = jnp.broadcast_to(extra, extra_ref.shape)
     owners = keep_ref.shape[0]
     for t in range(tiles):
         for j in range(2):
@@ -115,28 +91,57 @@
             send_ref[:, 2 * t + j, :] = jnp.where(core == 0, odd, even)
 
 
-def device_term(small_cols, wide_cols, token_counts, loss_sums, step):
+def device_term(small_cols, wide_cols, token_counts):
     tokens, width = small_cols.shape
     d = wide_cols.shape[2]
+    steps = tokens // STEP_TOKENS
     half = jax.ShapeDtypeStruct((width // 4, 2 * d // LANES, LANES), jnp.float32)
     return pl.pallas_call(
         term_kernel,
-        out_shape=(half, half, jax.ShapeDtypeStruct((8, LANES), jnp.float32)),
-        in_specs=[ANY] * 3 + [HBM] * 2,
-        out_specs=(VMEM, VMEM, VMEM),
+        out_shape=(half, half),
+        in_specs=[SMEM, HBM, HBM],
+        out_specs=(VMEM, VMEM),
         scratch_shapes=[
             pltpu.VMEM((tokens, width), jnp.bfloat16),
             pltpu.VMEM((tokens, 2, d), jnp.bfloat16),
+            pltpu.VMEM((width, 2 * tokens), jnp.bfloat16),
             pltpu.VMEM((d // LANES, width, LANES), jnp.float32),
-            pltpu.VMEM((1, 1), jnp.int32),
-            pltpu.VMEM((1, 1), jnp.float32),
-            pltpu.VMEM((1, 1), jnp.int32),
-            pltpu.SemaphoreType.DMA((tokens // STEP_TOKENS,)),
-            pltpu.SemaphoreType.DMA((4,)),
+            pltpu.SemaphoreType.DMA((steps,)),
+            pltpu.SemaphoreType.DMA,
         ],
         compiler_params=pltpu.CompilerParams(vmem_limit_bytes=16 * 2**20),
         name="term",
-    )(*(a.reshape(1, 1) for a in (token_counts, loss_sums, step)), in_hbm(small_cols), in_hbm(wide_cols))
+    )(token_counts, in_hbm(small_cols), in_hbm(wide_cols))
+
+
+def correction(step, log_beta):
+    u = step * log_beta
+    series = jnp.ones_like(u)
+    for k in range(11, 1, -1):
+        series = 1.0 + (u / k) * series
+    return jnp.where(u > -0.5, -u * series, 1.0 - jnp.exp(u))
+
+
+def chip_kernel(count_ref, loss_ref, step_ref, keep_ref, got_ref, sum_ref, extra_ref):
+    sum_ref[...] = keep_ref[...] + got_ref[...]
+    lane = lax.broadcasted_iota(jnp.int32, extra_ref.shape, 1)
+    scales = correction(step_ref[...], jnp.where(lane == 3, LOG_FIRST, LOG_SECOND))
+    count = count_ref[0].astype(jnp.float32)
+    extra_ref[...] = jnp.where(lane == 0, count, jnp.where(lane == 1, loss_ref[0], scales))
+
+
+def chip_sum(token_counts, loss_sums, step, keep, got):
+    return pl.pallas_call(
+        chip_kernel,
+        out_shape=(
+            jax.ShapeDtypeStruct(keep.shape, jnp.float32),
+            jax.ShapeDtypeStruct((8, LANES), jnp.float32),
+        ),
+        in_specs=[SMEM, SMEM, VMEM, VMEM, VMEM],
+        out_specs=(VMEM, VMEM),
+        compiler_params=pltpu.CompilerParams(vmem_limit_bytes=4 * 2**20),
+        name="chip",
+    )(token_counts, loss_sums, step, keep, got)
 
 
 def owned_kernel(extra_ref, parts_ref, out_ref):
@@ -247,11 +252,12 @@
     small_cols, wide_cols, token_counts, loss_sums, weight, first_moment, second_moment, step
 ):
     owners, replicas = lax.axis_size("fsdp"), lax.axis_size("dp")
-    keep, send, extra = device_term(small_cols, wide_cols, token_counts, loss_sums, step)
+    keep, send = device_term(small_cols, wide_cols, token_counts)
     partner = [(i, i ^ 1) for i in range(owners)]
-    chip_sum = keep + lax.ppermute(send, "fsdp", partner)
+    got = lax.ppermute(send, "fsdp", partner)
+    chip, extra = chip_sum(token_counts, loss_sums, jnp.broadcast_to(step.astype(jnp.float32), (8, LANES)), keep, got)
     same_core = [list(range(c, owners, 2)) for c in range(2)]
-    parts = lax.all_to_all(chip_sum, "fsdp", 0, 0, axis_index_groups=same_core, tiled=True)
+    parts = lax.all_to_all(chip, "fsdp", 0, 0, axis_index_groups=same_core, tiled=True)
     parts = lax.all_to_all(owned(extra, parts, replicas), "dp", 0, 0, tiled=True)
     summed, message = square(parts, owners)
     message = lax.all_to_all(message[:, None, :], "fsdp", 0, 0, tiled=True)[:, 0, :]

time: 72.1 us -> 69.3 us (0.961)
  Pallas kernels: 5.76 us -> 4.37 us
  waiting for transfers between devices: 1.33 us -> 0.03 us
    pallas_call x1 -> x2, Pallas kernels: 4.83 us -> 3.44 us  [the longest x1 3.38 us: device_term(): pl.pallas_call(term_kernel, out_shape=(half, half), in_specs=[SMEM, HBM,...]
    ppermute x1, waiting for transfers between devices: 1.33 us -> 0.03 us  [on_device(): got = lax.ppermute(send, 'fsdp', partner)]
  transfers between devices with their start and end apart: 1 -> 1, of which waited for: 1 -> 0; matrix products, arithmetic and copies ran while one was open for 0% -> 0% of each run, Pallas kernels for 0% -> 0%
where the time goes in v2:
time: 69.3 us; the launch traced here: 69 us
  blocking collectives  53.2 us (77%)
  starting transfers between devices  8.75 us (13%)
  Pallas kernels  4.37 us (6%)
  between operations  2.65 us (4%)
    all_to_all x1, blocking collectives, on_device(): lax.all_to_all(chip, 'fsdp', 0, 0, axis_index_groups=same_core, tiled=True)  18 us
    all_to_all x1, blocking collectives, on_device(): lax.all_to_all(owned(extra, parts, replicas), 'dp', 0, 0, tiled=True)  17.8 us
    all_to_all x1, blocking collectives, on_device(): lax.all_to_all(message[:, None, :], 'fsdp', 0, 0, tiled=True)[:, 0, :]  17.5 us
    ppermute x1, starting transfers between devices, on_device(): got = lax.ppermute(send, 'fsdp', partner)  8.75 us
    pallas_call x1, Pallas kernels, device_term(): pl.pallas_call(term_kernel, out_shape=(half, half), in_specs=[SMEM, HBM,...  3.38 us
  transfers between devices with their start and end apart: 1, of which 0 were waited for; matrix products, arithmetic and copies ran while one was open for 0% of the time, Pallas kernels for 0%

profile of v2, /device:TPU:1, one launch (start us, length us, event | category | flops | bytes accessed | tf_op | source)
XLA Modules:
  0.0 69.0 jit_solution(17828479958530945355)
XLA Ops:
  0.6 0.0 copy-start
  0.6 0.0 copy-start.1
  0.7 0.0 copy-start.2
  1.3 3.4 %term.1 = (f32[32,24,128]{2,1,0:T(8,128)S(1)}, f32[32,24,128]{2,1,0:T(8,128)S(1)}) custom-call(s32[1]{0:T(128)S(6)} %copy.15.count_ref, bf16[768,128]{1,0:T(8,128)(2,1)} %small_ref.1, bf16[768,2,1536]{2,1,0:T(2,128)(2,1)} %wide_ref.1), custom_call_target="tpu_custom_call" | custom-call | tf_op jit(solution)/shard_map/term/pallas_call | solution.py:99
  4.7 8.7 %collective-permute-start = (f32[32,24,128]{2,1,0:T(8,128)S(1)}, f32[32,24,128]{2,1,0:T(8,128)S(1)}, u32[]{:S(2)}, u32[]{:S(2)}) collective-permute-start(f32[32,24,128]{2,1,0:T(8,128)S(1)} %get-tuple-element.19), channel_id=1, source_target_pairs={{0,1},{1,0},{2,3},{3,2},{4,5},{5,4},{6,7},{7,6},{8,9},{9,8},{10,11... | collective-permute-start | bytes 1179656 | tf_op jit(solution)/shard_map/ppermute | solution.py:257
  14.8 0.0 collective-permute-done.got_ref
  14.8 0.1 chip.1
  14.9 18.0 %all_to_all.15.parts_ref = f32[32,24,128]{2,1,0:T(8,128)S(1)} all-to-all(f32[32,24,128]{2,1,0:T(8,128)S(1)} %get-tuple-element.21), channel_id=1, replica_groups={{0,2,4,6,8,10,12,14,16,18,20,22,24,26,28,30,32,34,36,38,40,42,44,46,48,..., dimensions={0} | all-to-all | bytes 786432 | tf_op jit(solution)/shard_map/all_to_all | solution.py:260
  32.9 17.8 %all_to_all.16.parts_ref = f32[8,32,128]{2,1,0:T(8,128)S(1)} all-to-all(f32[8,32,128]{2,1,0:T(8,128)S(1)} %owned.1), channel_id=1, replica_groups=mesh['dp'=8,'fsdp'=64] {'dp'}, dimensions={0} | all-to-all | bytes 262144 | tf_op jit(solution)/shard_map/all_to_all | solution.py:261
  50.7 0.1 square.1
  50.8 17.5 %all_to_all.17 = f32[64,1,128]{2,1,0:T(1,128)S(1)} all-to-all(f32[64,1,128]{2,1,0:T(1,128)S(1)} %bitcast.7), channel_id=1, replica_groups=mesh['dp'=8,'fsdp'=64] {'fsdp'}, dimensions={0} | all-to-all | bytes 65536 | tf_op jit(solution)/shard_map/all_to_all | solution.py:263
  68.3 0.0 copy-done
  68.3 0.0 copy-done.1
  68.3 0.0 copy-done.2
  68.3 0.8 %update.1 = (f32[2,1536]{1,0:T(2,128)}, f32[2,1536]{1,0:T(2,128)}, f32[2,1536]{1,0:T(2,128)}, f32[2,1536]{1,0:T(2,128)}, f32[1,1]{1,0:T(1,128)}, /*index=5*/f32[1,1]{1,0:T(1,128)}) custom-call(f32[8,128]{1,0:T(8,128)S(1)} %get-tuple-element.20.extra_ref, f32[64,128]{1,0:T(8,128)S(1)} %bitcast.6, f32[24,128]{1,0:T(8,128)S(1)} %get-tuple-element.23.summed_ref, ...), custom_call_target="tpu_custom_call" | custom-call | tf_op jit(solution)/shard_map/update/pallas_call | solution.py:240
  (2 shorter events, 0.0 us)
Async XLA Ops:
  0.6 67.7 %copy-start = (f32[2,1536]{1,0:T(2,128)S(1)}, f32[2,1536]{1,0:T(2,128)}, u32[]{:S(2)}) copy-start(f32[2,1536]{1,0:T(2,128)} %weight_ref.1) | copy-start | bytes 36868
  0.6 67.6 %copy-start.1 = (f32[2,1536]{1,0:T(2,128)S(1)}, f32[2,1536]{1,0:T(2,128)}, u32[]{:S(2)}) copy-start(f32[2,1536]{1,0:T(2,128)} %first_ref.1) | copy-start | bytes 36868
  0.7 67.6 %copy-start.2 = (f32[2,1536]{1,0:T(2,128)S(1)}, f32[2,1536]{1,0:T(2,128)}, u32[]{:S(2)}) copy-start(f32[2,1536]{1,0:T(2,128)} %second_ref.1) | copy-start | bytes 36868
  4.7 10.1 %collective-permute-start = (f32[32,24,128]{2,1,0:T(8,128)S(1)}, f32[32,24,128]{2,1,0:T(8,128)S(1)}, u32[]{:S(2)}, u32[]{:S(2)}) collective-permute-start(f32[32,24,128]{2,1,0:T(8,128)S(1)} %get-tuple-element.19), channel_id=1, source_target_pairs={{0,1},{1,0},{2,3},{3,2},{4,5},{5,4},{6,7},{7,6},{8,9},{9,8},{10,11... | collective-permute-start | bytes 1179656 | tf_op jit(solution)/shard_map/ppermute | solution.py:257

commit v3 on v2

--- a/solution.py
+++ b/solution.py
@@ -146,18 +146,20 @@
 
 def owned_kernel(extra_ref, parts_ref, out_ref):
     rows = parts_ref.shape[1]
+    replicas = out_ref.shape[0]
     total = jnp.sum(parts_ref[...], axis=0)
-    extra = extra_ref[...]
-    for k in range(out_ref.shape[0]):
-        out_ref[k, 0:rows, :] = total
-        out_ref[k, rows:, :] = extra
+    for r in range(rows):
+        row = jnp.broadcast_to(total[r : r + 1][None], (replicas, 1, LANES))
+        out_ref[:, :, r * LANES : (r + 1) * LANES] = row
+    row = jnp.broadcast_to(extra_ref[0:1][None], (replicas, 1, LANES))
+    out_ref[:, :, rows * LANES :] = row
 
 
 def owned(extra, parts, replicas):
-    rows = parts.shape[1] + extra.shape[0]
+    columns = (parts.shape[1] + 1) * LANES
     return pl.pallas_call(
         owned_kernel,
-        out_shape=jax.ShapeDtypeStruct((replicas, rows, LANES), jnp.float32),
+        out_shape=jax.ShapeDtypeStruct((replicas, 1, columns), jnp.float32),
         in_specs=[VMEM, VMEM],
         out_specs=VMEM,
         compiler_params=pltpu.CompilerParams(vmem_limit_bytes=4 * 2**20),
@@ -167,18 +169,19 @@
 
 def square_kernel(parts_ref, summed_ref, message_ref):
     rows = summed_ref.shape[0]
-    total = jnp.sum(parts_ref[...], axis=0)
-    summed = total[:rows]
-    summed_ref[...] = summed
+    for r in range(rows):
+        part = parts_ref[:, :, r * LANES : (r + 1) * LANES]
+        summed_ref[r : r + 1, :] = jnp.sum(part, axis=0)
+    summed = summed_ref[...]
     squares = jnp.sum(summed * summed)
     lane = lax.broadcasted_iota(jnp.int32, (1, LANES), 1)
-    shifted = total[rows : rows + 1]
+    shifted = jnp.sum(parts_ref[:, :, rows * LANES :], axis=0)
     message = jnp.where(lane == 2, squares, shifted)
     message_ref[...] = jnp.broadcast_to(message, message_ref.shape)
 
 
 def square(parts, owners):
-    rows = parts.shape[1] - 8
+    rows = parts.shape[2] // LANES - 1
     return pl.pallas_call(
         square_kernel,
         out_shape=(

time: 69.3 us -> 69.1 us (level)
  no operation moved by 1% of the time
where the time goes in v3:
time: 69.1 us; the launch traced here: 68.8 us
  blocking collectives  52.9 us (77%)
  starting transfers between devices  8.75 us (13%)
  Pallas kernels  4.47 us (6%)
  between operations  2.65 us (4%)
    all_to_all x1, blocking collectives, on_device(): lax.all_to_all(chip, 'fsdp', 0, 0, axis_index_groups=same_core, tiled=True)  18 us
    all_to_all x1, blocking collectives, on_device(): lax.all_to_all(message[:, None, :], 'fsdp', 0, 0, tiled=True)[:, 0, :]  17.5 us
    all_to_all x1, blocking collectives, on_device(): lax.all_to_all(owned(extra, parts, replicas), 'dp', 0, 0, tiled=True)  17.5 us
    ppermute x1, starting transfers between devices, on_device(): got = lax.ppermute(send, 'fsdp', partner)  8.75 us
    pallas_call x1, Pallas kernels, device_term(): pl.pallas_call(term_kernel, out_shape=(half, half), in_specs=[SMEM, HBM,...  3.38 us
  transfers between devices with their start and end apart: 1, of which 0 were waited for; matrix products, arithmetic and copies ran while one was open for 0% of the time, Pallas kernels for 0%

profile of v3, /device:TPU:1, one launch (start us, length us, event | category | flops | bytes accessed | tf_op | source)
XLA Modules:
  0.0 68.8 jit_solution(800584276278006384)
XLA Ops:
  0.6 0.0 copy-start
  0.6 0.0 copy-start.1
  0.7 0.0 copy-start.2
  1.3 3.4 %term.1 = (f32[32,24,128]{2,1,0:T(8,128)S(1)}, f32[32,24,128]{2,1,0:T(8,128)S(1)}) custom-call(s32[1]{0:T(128)S(6)} %copy.15.count_ref, bf16[768,128]{1,0:T(8,128)(2,1)} %small_ref.1, bf16[768,2,1536]{2,1,0:T(2,128)(2,1)} %wide_ref.1), custom_call_target="tpu_custom_call" | custom-call | tf_op jit(solution)/shard_map/term/pallas_call | solution.py:99
  4.7 8.7 %collective-permute-start = (f32[32,24,128]{2,1,0:T(8,128)S(1)}, f32[32,24,128]{2,1,0:T(8,128)S(1)}, u32[]{:S(2)}, u32[]{:S(2)}) collective-permute-start(f32[32,24,128]{2,1,0:T(8,128)S(1)} %get-tuple-element.19), channel_id=1, source_target_pairs={{0,1},{1,0},{2,3},{3,2},{4,5},{5,4},{6,7},{7,6},{8,9},{9,8},{10,11... | collective-permute-start | bytes 1179656 | tf_op jit(solution)/shard_map/ppermute | solution.py:260
  14.8 0.0 collective-permute-done.got_ref
  14.8 0.1 chip.1
  14.9 18.0 %all_to_all.15.parts_ref = f32[32,24,128]{2,1,0:T(8,128)S(1)} all-to-all(f32[32,24,128]{2,1,0:T(8,128)S(1)} %get-tuple-element.21), channel_id=1, replica_groups={{0,2,4,6,8,10,12,14,16,18,20,22,24,26,28,30,32,34,36,38,40,42,44,46,48,..., dimensions={0} | all-to-all | bytes 786432 | tf_op jit(solution)/shard_map/all_to_all | solution.py:263
  32.9 0.1 owned.1
  33.0 17.5 %all_to_all.16.parts_ref = f32[8,1,3200]{2,1,0:T(1,128)S(1)} all-to-all(f32[8,1,3200]{2,1,0:T(1,128)S(1)} %owned.1), channel_id=1, replica_groups=mesh['dp'=8,'fsdp'=64] {'dp'}, dimensions={0} | all-to-all | bytes 204800 | tf_op jit(solution)/shard_map/all_to_all | solution.py:264
  50.4 0.2 square.1
  50.6 17.5 %all_to_all.17 = f32[64,1,128]{2,1,0:T(1,128)S(1)} all-to-all(f32[64,1,128]{2,1,0:T(1,128)S(1)} %bitcast.7), channel_id=1, replica_groups=mesh['dp'=8,'fsdp'=64] {'fsdp'}, dimensions={0} | all-to-all | bytes 65536 | tf_op jit(solution)/shard_map/all_to_all | solution.py:266
  68.1 0.0 copy-done
  68.1 0.0 copy-done.1
  68.1 0.0 copy-done.2
  68.1 0.8 %update.1 = (f32[2,1536]{1,0:T(2,128)}, f32[2,1536]{1,0:T(2,128)}, f32[2,1536]{1,0:T(2,128)}, f32[2,1536]{1,0:T(2,128)}, f32[1,1]{1,0:T(1,128)}, /*index=5*/f32[1,1]{1,0:T(1,128)}) custom-call(f32[8,128]{1,0:T(8,128)S(1)} %get-tuple-element.20.extra_ref, f32[64,128]{1,0:T(8,128)S(1)} %bitcast.6, f32[24,128]{1,0:T(8,128)S(1)} %get-tuple-element.23.summed_ref, ...), custom_call_target="tpu_custom_call" | custom-call | tf_op jit(solution)/shard_map/update/pallas_call | solution.py:243
  (1 shorter events, 0.0 us)
Async XLA Ops:
  0.6 67.4 %copy-start = (f32[2,1536]{1,0:T(2,128)S(1)}, f32[2,1536]{1,0:T(2,128)}, u32[]{:S(2)}) copy-start(f32[2,1536]{1,0:T(2,128)} %weight_ref.1) | copy-start | bytes 36868
  0.6 67.4 %copy-start.1 = (f32[2,1536]{1,0:T(2,128)S(1)}, f32[2,1536]{1,0:T(2,128)}, u32[]{:S(2)}) copy-start(f32[2,1536]{1,0:T(2,128)} %first_ref.1) | copy-start | bytes 36868
  0.7 67.4 %copy-start.2 = (f32[2,1536]{1,0:T(2,128)S(1)}, f32[2,1536]{1,0:T(2,128)}, u32[]{:S(2)}) copy-start(f32[2,1536]{1,0:T(2,128)} %second_ref.1) | copy-start | bytes 36868
  4.7 10.1 %collective-permute-start = (f32[32,24,128]{2,1,0:T(8,128)S(1)}, f32[32,24,128]{2,1,0:T(8,128)S(1)}, u32[]{:S(2)}, u32[]{:S(2)}) collective-permute-start(f32[32,24,128]{2,1,0:T(8,128)S(1)} %get-tuple-element.19), channel_id=1, source_target_pairs={{0,1},{1,0},{2,3},{3,2},{4,5},{5,4},{6,7},{7,6},{8,9},{9,8},{10,11... | collective-permute-start | bytes 1179656 | tf_op jit(solution)/shard_map/ppermute | solution.py:260

commit v4 on v3

--- a/solution.py
+++ b/solution.py
@@ -32,12 +32,11 @@
     count_ref,
     small_ref,
     wide_ref,
-    keep_ref,
+    total_ref,
     send_ref,
     small_vmem,
     wide_vmem,
     narrow,
-    total,
     sems,
     small_sem,
 ):
@@ -72,7 +71,7 @@
         slot = lax.broadcasted_iota(jnp.int32, (width, 2 * block), 1)
         rows = jnp.where(slot % 2 == row // (width // 2), rows, 0.0)
         narrow[:, 2 * block * i : 2 * block * (i + 1)] = rows.astype(jnp.bfloat16)
-    tiles = total.shape[0]
+    tiles = total_ref.shape[1]
     for i in range(steps):
         copies[i].wait()
         broad = wide_vmem[i * each : (i + 1) * each].reshape(2 * each, tiles * LANES)
@@ -80,15 +79,34 @@
             narrow[:, 2 * each * i : 2 * each * (i + 1)], broad, preferred_element_type=jnp.float32
         )
         for t in range(tiles):
-            part = term[:, t * LANES : (t + 1) * LANES]
-            total[t] = part if i == 0 else total[t] + part
-    owners = keep_ref.shape[0]
-    for t in range(tiles):
+            total_ref[i, t] = term[:, t * LANES : (t + 1) * LANES]
+    take_half(total_ref, 1 - core, send_ref)
+
+
+def take_half(total_ref, column, half_ref):
+    owners = half_ref.shape[0]
+    for t in range(total_ref.shape[1]):
         for j in range(2):
-            even = total[t, pl.ds(j, owners, stride=4), :]
-            odd = total[t, pl.ds(2 + j, owners, stride=4), :]
-            keep_ref[:, 2 * t + j, :] = jnp.where(core == 0, even, odd)
-            send_ref[:, 2 * t + j, :] = jnp.where(core == 0, odd, even)
+            rows = pl.ds(2 * column + j, owners, stride=4)
+            half_ref[:, 2 * t + j, :] = sum(
+                total_ref[i, t, rows, :] for i in range(total_ref.shape[0])
+            )
+
+
+def keep_kernel(total_ref, keep_ref):
+    take_half(total_ref, lax.rem(lax.axis_index("fsdp"), 2), keep_ref)
+
+
+def kept(total, half):
+    return pl.pallas_call(
+        keep_kernel,
+        out_shape=jax.ShapeDtypeStruct(half.shape, half.dtype),
+        in_specs=[VMEM],
+        out_specs=VMEM,
+        cost_estimate=pl.CostEstimate(flops=10**8, bytes_accessed=10**6, transcendentals=0),
+        compiler_params=pltpu.CompilerParams(vmem_limit_bytes=4 * 2**20),
+        name="keep",
+    )(total)
 
 
 def device_term(small_cols, wide_cols, token_counts):
@@ -98,14 +116,16 @@
     half = jax.ShapeDtypeStruct((width // 4, 2 * d // LANES, LANES), jnp.float32)
     return pl.pallas_call(
         term_kernel,
-        out_shape=(half, half),
+        out_shape=(
+            jax.ShapeDtypeStruct((steps, d // LANES, width, LANES), jnp.float32),
+            half,
+        ),
         in_specs=[SMEM, HBM, HBM],
         out_specs=(VMEM, VMEM),
         scratch_shapes=[
             pltpu.VMEM((tokens, width), jnp.bfloat16),
             pltpu.VMEM((tokens, 2, d), jnp.bfloat16),
             pltpu.VMEM((width, 2 * tokens), jnp.bfloat16),
-            pltpu.VMEM((d // LANES, width, LANES), jnp.float32),
             pltpu.SemaphoreType.DMA((steps,)),
             pltpu.SemaphoreType.DMA,
         ],
@@ -255,9 +275,10 @@
     small_cols, wide_cols, token_counts, loss_sums, weight, first_moment, second_moment, step
 ):
     owners, replicas = lax.axis_size("fsdp"), lax.axis_size("dp")
-    keep, send = device_term(small_cols, wide_cols, token_counts)
+    total, send = device_term(small_cols, wide_cols, token_counts)
     partner = [(i, i ^ 1) for i in range(owners)]
     got = lax.ppermute(send, "fsdp", partner)
+    keep = kept(total, send)
     chip, extra = chip_sum(token_counts, loss_sums, jnp.broadcast_to(step.astype(jnp.float32), (8, LANES)), keep, got)
     same_core = [list(range(c, owners, 2)) for c in range(2)]
     parts = lax.all_to_all(chip, "fsdp", 0, 0, axis_index_groups=same_core, tiled=True)

time: 69.1 us -> 69.3 us (level)
    pallas_call x1 -> x2, Pallas kernels: 3.38 us -> 3.5 us  [the longest x1 3.25 us: device_term(): pl.pallas_call(term_kernel, out_shape=(jax.ShapeDtypeStruct((steps, d //...]
where the time goes in v4:
time: 69.3 us; the launch traced here: 69 us
  blocking collectives  52.9 us (76%)
  starting transfers between devices  8.74 us (13%)
  Pallas kernels  4.6 us (7%)
  between operations  2.68 us (4%)
    all_to_all x1, blocking collectives, on_device(): lax.all_to_all(chip, 'fsdp', 0, 0, axis_index_groups=same_core, tiled=True)  18.5 us
    all_to_all x1, blocking collectives, on_device(): lax.all_to_all(owned(extra, parts, replicas), 'dp', 0, 0, tiled=True)  17.6 us
    all_to_all x1, blocking collectives, on_device(): lax.all_to_all(message[:, None, :], 'fsdp', 0, 0, tiled=True)[:, 0, :]  16.9 us
    ppermute x1, starting transfers between devices, on_device(): got = lax.ppermute(send, 'fsdp', partner)  8.74 us
    pallas_call x1, Pallas kernels, device_term(): pl.pallas_call(term_kernel, out_shape=(jax.ShapeDtypeStruct((steps, d //...  3.25 us
  transfers between devices with their start and end apart: 1, of which 0 were waited for; matrix products, arithmetic and copies ran while one was open for 0% of the time, Pallas kernels for 0%

profile of v4, /device:TPU:1, one launch (start us, length us, event | category | flops | bytes accessed | tf_op | source)
XLA Modules:
  0.0 69.0 jit_solution(5500662301815092828)
XLA Ops:
  0.6 0.0 copy-start.2
  0.6 0.0 copy-start.1
  0.7 0.0 copy-start
  1.3 3.3 %term.1 = (f32[2,12,128,128]{3,2,1,0:T(8,128)S(1)}, f32[32,24,128]{2,1,0:T(8,128)S(1)}) custom-call(s32[1]{0:T(128)S(6)} %copy.15.count_ref, bf16[768,128]{1,0:T(8,128)(2,1)} %small_ref.1, bf16[768,2,1536]{2,1,0:T(2,128)(2,1)} %wide_ref.1), custom_call_target="tpu_custom_call" | custom-call | tf_op jit(solution)/shard_map/term/pallas_call | solution.py:117
  4.6 8.7 %collective-permute-start = (f32[32,24,128]{2,1,0:T(8,128)S(1)}, f32[32,24,128]{2,1,0:T(8,128)S(1)}, u32[]{:S(2)}, u32[]{:S(2)}) collective-permute-start(f32[32,24,128]{2,1,0:T(8,128)S(1)} %get-tuple-element.19), channel_id=1, source_target_pairs={{0,1},{1,0},{2,3},{3,2},{4,5},{5,4},{6,7},{7,6},{8,9},{9,8},{10,11... | collective-permute-start | bytes 1179656 | tf_op jit(solution)/shard_map/ppermute | solution.py:280
  14.6 0.2 keep.1.keep_ref
  14.9 0.0 collective-permute-done.got_ref
  14.9 0.1 chip.1
  15.0 18.5 %all_to_all.15.parts_ref = f32[32,24,128]{2,1,0:T(8,128)S(1)} all-to-all(f32[32,24,128]{2,1,0:T(8,128)S(1)} %get-tuple-element.21), channel_id=1, replica_groups={{0,2,4,6,8,10,12,14,16,18,20,22,24,26,28,30,32,34,36,38,40,42,44,46,48,..., dimensions={0} | all-to-all | bytes 786432 | tf_op jit(solution)/shard_map/all_to_all | solution.py:284
  33.5 0.1 owned.1
  33.6 17.6 %all_to_all.16.parts_ref = f32[8,1,3200]{2,1,0:T(1,128)S(1)} all-to-all(f32[8,1,3200]{2,1,0:T(1,128)S(1)} %owned.1), channel_id=1, replica_groups=mesh['dp'=8,'fsdp'=64] {'dp'}, dimensions={0} | all-to-all | bytes 204800 | tf_op jit(solution)/shard_map/all_to_all | solution.py:285
  51.1 0.2 square.1
  51.3 16.9 %all_to_all.17 = f32[64,1,128]{2,1,0:T(1,128)S(1)} all-to-all(f32[64,1,128]{2,1,0:T(1,128)S(1)} %bitcast.7), channel_id=1, replica_groups=mesh['dp'=8,'fsdp'=64] {'fsdp'}, dimensions={0} | all-to-all | bytes 65536 | tf_op jit(solution)/shard_map/all_to_all | solution.py:287
  68.2 0.0 copy-done.2
  68.2 0.0 copy-done.1
  68.2 0.0 copy-done
  68.2 0.8 %update.1 = (f32[2,1536]{1,0:T(2,128)}, f32[2,1536]{1,0:T(2,128)}, f32[2,1536]{1,0:T(2,128)}, f32[2,1536]{1,0:T(2,128)}, f32[1,1]{1,0:T(1,128)}, /*index=5*/f32[1,1]{1,0:T(1,128)}) custom-call(f32[8,128]{1,0:T(8,128)S(1)} %get-tuple-element.20.extra_ref, f32[64,128]{1,0:T(8,128)S(1)} %bitcast.6, f32[24,128]{1,0:T(8,128)S(1)} %get-tuple-element.23.summed_ref, ...), custom_call_target="tpu_custom_call" | custom-call | tf_op jit(solution)/shard_map/update/pallas_call | solution.py:263
  (1 shorter events, 0.0 us)
Async XLA Ops:
  0.6 67.6 %copy-start.2 = (f32[2,1536]{1,0:T(2,128)S(1)}, f32[2,1536]{1,0:T(2,128)}, u32[]{:S(2)}) copy-start(f32[2,1536]{1,0:T(2,128)} %second_ref.1) | copy-start | bytes 36868
  0.6 67.6 %copy-start.1 = (f32[2,1536]{1,0:T(2,128)S(1)}, f32[2,1536]{1,0:T(2,128)}, u32[]{:S(2)}) copy-start(f32[2,1536]{1,0:T(2,128)} %first_ref.1) | copy-start | bytes 36868
  0.7 67.6 %copy-start = (f32[2,1536]{1,0:T(2,128)S(1)}, f32[2,1536]{1,0:T(2,128)}, u32[]{:S(2)}) copy-start(f32[2,1536]{1,0:T(2,128)} %weight_ref.1) | copy-start | bytes 36868
  4.6 10.3 %collective-permute-start = (f32[32,24,128]{2,1,0:T(8,128)S(1)}, f32[32,24,128]{2,1,0:T(8,128)S(1)}, u32[]{:S(2)}, u32[]{:S(2)}) collective-permute-start(f32[32,24,128]{2,1,0:T(8,128)S(1)} %get-tuple-element.19), channel_id=1, source_target_pairs={{0,1},{1,0},{2,3},{3,2},{4,5},{5,4},{6,7},{7,6},{8,9},{9,8},{10,11... | collective-permute-start | bytes 1179656 | tf_op jit(solution)/shard_map/ppermute | solution.py:280
